TPU v7x, 32 devices: a whole 2x2x4 slice. The times are simulated.
32 devices in a mesh: tile: 16 (over z, y, x), member: 2 (over core).
Axes of the slice: x: 2, y: 2, z: 4, core: 2. Of those that a mesh axis runs over, the one named last changes fastest.
Arguments:
- pixels: bfloat16 [96, 400, 1152], P('tile', 'member'), parts along dimension 1, may hold values from -6 to 6
- channel_index_table: int32 [16, 6], P('tile'), may hold values from 0 to 68, as said below
- group_sizes: int32 [16], P('tile'), may hold values from 0 to 6, as said below
- patch_weight: bfloat16 [9, 200, 512], replicated, may hold values from -0.4375 to 0.4375
- patch_bias: bfloat16 [9, 512], replicated, may hold values from -3 to 3
- level_code: bfloat16 [14, 512], replicated, may hold values from -3 to 3
- latents: bfloat16 [3, 512], replicated
- perc_query: bfloat16 [512, 512], replicated, may hold values from -0.25 to 0.25
- perc_kv: bfloat16 [512, 1024], replicated, may hold values from -0.25 to 0.25
- perc_out: bfloat16 [512, 512], replicated, may hold values from -0.25 to 0.25
- norm_gain: bfloat16 [512], replicated, may hold values from 0.5 to 1.5
- window_qkv: bfloat16 [512, 1536], replicated
- window_out: bfloat16 [512, 512], replicated, may hold values from -0.25 to 0.25
- shift: int32 [1], replicated, may hold values from 1 to 11
Outputs:
- encoded: bfloat16 [4, 16, 12, 12, 512], P(None, 'tile', 'member'), parts along dimension 2
There are 2 independent parts, one for each index of `member`. A program takes and returns all parts, laid end to end along the dimension named above; an argument that names none is the same for every part. Nothing has to cross between parts.
Inputs may be any that keep to these rules, and one draw needn't show every extreme that they name: `channel_index_table`: slots 0 to group_sizes - 1 of the devices hold distinct channels, and together every one of the 69 channels once; channel c < 65 is variable c // 13 at level c % 13, the others are surface variables; other slots hold any channel number. `group_sizes`: they sum to 69; some device holds 6.
All inputs are finite; a program needn't handle non-finite values.
Results may differ from a plain program's by a relative error of at most 0.0095.
Values may be sent and summed in bfloat16 or wider, within the bound.
A program may use at most 128 MiB of HBM per device.

v0:
```python
import math

import jax
import jax.numpy as jnp
from jax import lax
from jax.sharding import PartitionSpec as P

LEVELS = 13
V_ATM = 5
LATENT = 3
HEADS = 8
WL = 2
WH = 6
WW = 12
LT = 8


def passed_along(block, axis, distance):
    devices = range(lax.axis_size(axis))
    route = [((i - distance) % len(devices), i) for i in devices]
    return lax.ppermute(block, axis, route)


def layer_norm(values, norm_gain):
    center = values - jnp.mean(values, axis=-1, keepdims=True)
    spread = jnp.mean(center * center, axis=-1, keepdims=True)
    return center * lax.rsqrt(spread + 1e-05) * norm_gain.astype(jnp.float32)


def embed_slots(raw_slots, slot_ids, patch_weight, patch_bias):
    count, values_per, patches = raw_slots.shape
    kind_count = patch_weight.shape[0]
    width = patch_weight.shape[2]
    block = math.gcd(count, 16)
    kinds = jnp.where(
        slot_ids < V_ATM * LEVELS, slot_ids // LEVELS, slot_ids - V_ATM * LEVELS + V_ATM
    )
    picker = (kinds[:, None] == jnp.arange(kind_count, dtype=jnp.int32)[None, :]).astype(
        jnp.bfloat16
    )
    raw_blocks = raw_slots.reshape(count // block, block, values_per, patches)
    pick_blocks = picker.reshape(count // block, block, kind_count)

    def one_block(packed):
        unprocessed_part, pick_piece = packed
        chosen_weight = jnp.einsum(
            "lk,kqt->lqt", pick_piece, patch_weight, preferred_element_type=jnp.float32
        ).astype(jnp.bfloat16)
        biases = jnp.dot(pick_piece, patch_bias, preferred_element_type=jnp.float32)
        embedded = jnp.einsum(
            "lqd,lqt->ldt", unprocessed_part, chosen_weight, preferred_element_type=jnp.float32
        )
        return (embedded + biases[:, None, :]).astype(jnp.bfloat16)

    result = lax.map(one_block, (raw_blocks, pick_blocks))
    return result.reshape(count, patches, width)


def perceive(level_tokens, latents, perc_query, perc_kv, perc_out):
    count_levels, patch_count, width = level_tokens.shape
    head_size = width // HEADS
    pair = jnp.dot(
        level_tokens.reshape(-1, width), perc_kv, preferred_element_type=jnp.float32
    ).astype(jnp.bfloat16)
    pair = pair.reshape(count_levels, patch_count, 2, HEADS, head_size)
    query = jnp.dot(latents, perc_query, preferred_element_type=jnp.float32).reshape(
        LATENT, HEADS, head_size
    )
    attention_logits = jnp.einsum(
        "jhd,lphd->jphl", query, pair[:, :, 0].astype(jnp.float32)
    ) / math.sqrt(head_size)
    attn_b = jax.nn.softmax(attention_logits, axis=-1).astype(jnp.bfloat16)
    gathered = jnp.einsum(
        "jphl,lphd->jphd", attn_b, pair[:, :, 1], preferred_element_type=jnp.float32
    )
    gathered = gathered.astype(jnp.bfloat16).reshape(LATENT * patch_count, width)
    projected = jnp.dot(gathered, perc_out, preferred_element_type=jnp.float32).reshape(
        LATENT, patch_count, width
    )
    return latents.astype(jnp.float32)[:, None, :] + projected


def window_attend(packed):
    count_windows, members, triple_width = packed.shape
    width = triple_width // 3
    head_size = width // HEADS
    split = packed.reshape(count_windows, members, 3, HEADS, head_size)
    logits = jnp.einsum(
        "wqhd,wkhd->whqk", split[:, :, 0], split[:, :, 1], preferred_element_type=jnp.float32
    ) / math.sqrt(head_size)
    attention_weight = jax.nn.softmax(logits, axis=-1).astype(jnp.bfloat16)
    mixed = jnp.einsum(
        "whqk,wkhd->wqhd", attention_weight, split[:, :, 2], preferred_element_type=jnp.float32
    )
    return mixed.astype(jnp.bfloat16).reshape(count_windows, members, width)


def local(
    pixels,
    channel_index_table,
    group_sizes,
    patch_weight,
    patch_bias,
    level_code,
    latents,
    perc_query,
    perc_kv,
    perc_out,
    norm_gain,
    window_qkv,
    window_out,
    shift,
):
    tiles = lax.axis_size("tile")
    bands = tiles // LT
    slots_dev = pixels.shape[0]
    patches_dev = pixels.shape[2] // tiles
    width = patch_weight.shape[2]
    all_ids, all_sizes = (
        lax.all_gather(channel_index_table, "tile", axis=0, tiled=True),
        lax.all_gather(group_sizes, "tile", axis=0, tiled=True),
    )
    slot_ids = all_ids.reshape(-1)
    received = lax.all_to_all(pixels, "tile", split_axis=2, concat_axis=0, tiled=True)
    embedded = embed_slots(received, slot_ids, patch_weight, patch_bias)
    live = (jnp.arange(slots_dev, dtype=jnp.int32)[None, :] < all_sizes[:, None]).reshape(-1)
    level_of = jnp.where(slot_ids < V_ATM * LEVELS, slot_ids % LEVELS, LEVELS)
    selector = (
        (level_of[None, :] == jnp.arange(LEVELS + 1, dtype=jnp.int32)[:, None]) & live[None, :]
    ).astype(jnp.bfloat16)
    level_sum = jnp.einsum("ls,spe->lpe", selector, embedded, preferred_element_type=jnp.float32)
    codes = level_code.astype(jnp.float32)
    level_tokens = (level_sum[:LEVELS] + codes[:LEVELS, None, :]).astype(jnp.bfloat16)
    surface = level_sum[LEVELS] + codes[LEVELS]
    latent_state = perceive(level_tokens, latents, perc_query, perc_kv, perc_out)
    columns = patches_dev // WH
    state = jnp.concatenate([latent_state, surface[None]], axis=0).reshape(
        LATENT + 1, WH, columns, width
    )
    normed = layer_norm(state, norm_gain).astype(jnp.bfloat16)
    rims = []
    for distance, rim_piece in ((bands, normed), (-bands, normed)):
        rims.append(passed_along(rim_piece, "tile", distance))
    extended = jnp.concatenate([rims[0], normed, rims[1]], axis=2)
    offset = shift[0]
    span = columns + WW
    shifted = lax.dynamic_slice_in_dim(extended, offset, span, 2)
    count_windows = span // WW
    level_groups = (LATENT + 1) // WL
    windowed = shifted.reshape(level_groups, WL, WH, count_windows, WW, width).transpose(
        0, 3, 1, 2, 4, 5
    )
    triple = jnp.dot(
        windowed.reshape(-1, width), window_qkv, preferred_element_type=jnp.float32
    ).astype(jnp.bfloat16)
    triple = triple.reshape(level_groups * count_windows, WL * WH * WW, 3 * width)
    mixed = window_attend(triple)
    mixed = (
        mixed.reshape(level_groups, count_windows, WL, WH, WW, width)
        .transpose(0, 2, 3, 1, 4, 5)
        .reshape(LATENT + 1, WH, span, width)
    )
    own_mixed = lax.dynamic_slice_in_dim(mixed, WW - offset, columns, 2)
    projected = jnp.dot(
        own_mixed.reshape(-1, width), window_out, preferred_element_type=jnp.float32
    ).reshape(state.shape)
    return (state + projected).astype(jnp.bfloat16)[:, None]


def solution(mesh):
    in_specs = (
        P("tile", "member", None),
        P("tile", None),
        P("tile"),
        P(),
        P(),
        P(),
        P(),
        P(),
        P(),
        P(),
        P(),
        P(),
        P(),
        P(),
    )
    out_specs = P(None, "tile", "member", None, None)
    return jax.shard_map(local, mesh=mesh, in_specs=in_specs, out_specs=out_specs, check_vma=False)
```

profile of v0, /device:TPU:12, one launch (start us, length us, event | category | flops | bytes accessed | tf_op | source)
XLA Modules:
  0.0 305.9 jit_solution(16971263444059298851)
XLA Ops:
  0.0 6.8 %copy.72 = bf16[6,200,1152]{1,0,2:T(8,128)(2,1)} copy(bf16[6,200,1152]{2,1,0:T(8,128)(2,1)} %param.16) | data formatting | bytes 5529600 | tf_op args[0]
  6.8 7.3 %all-to-all-start = ((bf16[6,200,1152]{1,0,2:T(8,128)(2,1)}), bf16[6,200,1152]{1,0,2:T(8,128)(2,1)}, u32[]{:S(2)}, u32[]{:S(2)}) async-start(bf16[6,200,1152]{1,0,2:T(8,128)(2,1)} %copy.72), calls=%async_computation | async-start | bytes 9437184 | tf_op jit(solution)/shard_map/all_to_all | solution.py:124
  14.2 127.6 %all-gather = s32[16,1,6]{2,1,0:T(1,128)S(1)} all-gather(s32[1,1,6]{2,1,0:T(1,128)S(1)} %bitcast.114), channel_id=1, replica_groups=mesh['tile'=16,'member'=2] {'tile'}, dimensions={0}, use_global_device_ids=true | all-gather | bytes 408 | tf_op jit(solution)/shard_map/all_gather | solution.py:120
  142.5 2.6 copy.75
  147.2 13.7 %all-reduce = s32[16]{0:T(128)S(1)} all-reduce(s32[16]{0:T(128)S(1)} %dynamic-update-slice), channel_id=1, replica_groups=mesh['tile'=16,'member'=2] {'tile'}, use_global_device_ids=true, to_apply=%add | all-reduce | flops 16 | bytes 128
  161.1 1.2 fusion.69
  162.5 5.0 %copy.74 = bf16[16,6,200,72]{2,3,1,0:T(8,128)(2,1)} copy(bf16[16,6,200,72]{2,1,3,0:T(8,128)(2,1)} %bitcast.9) | data formatting | bytes 5529600 | tf_op jit(solution)/shard_map/all_to_all | solution.py:124
  167.6 53.3 %while.10 = (s32[]{:T(128)}, bf16[6,16,72,512]{3,2,1,0:T(8,128)(2,1)}, bf16[6,16,200,72]{2,3,1,0:T(8,128)(2,1)}, bf16[6,16,9]{2,1,0:T(8,128)(2,1)S(1)}, bf16[9,2...) while((s32[]{:T(128)}, bf16[6,16,72,512]{3,2,1,0:T(8,128)(2,1)}, ...), condition=%wide.region_1.2_spmd, body=%wide.region_0.1_spmd.sunk | while | flops 268386304 | bytes 10257493 | solution.py:55
  167.6 2.9 convolution_convert_fusion.4
  170.6 5.8 %fusion.95 = bf16[6,16,72,512]{3,2,1,0:T(8,128)(2,1)} fusion(bf16[6,16,72,512]{3,2,1,0:T(8,128)(2,1)} %get-tuple-element.121, s32[]{:T(128)} %get-tuple-element.120, bf16[16,200,512]{2,0,1:T(8,128)(2,1)S(1)} %convolution_convert_fusion.4, f32[16,512]{1,0:T(8,128)S(1)} %fusion.94, bf16[6,16,200,72]{2,3,1,0:T(8,128)(2,1)} %get-tuple-element.129), kind=kOutput, calls=%fused_computation.5.clone.1 | convolution fusion | flops 237109248 | bytes 5080064 | tf_op jit(solution)/shard_map/while/body/eval_jaxpr/lqd,lqt->ldt/dot_general | solution.py:50
  176.4 2.9 convolution_convert_fusion.4
  179.5 5.9 %fusion.95 = bf16[6,16,72,512]{3,2,1,0:T(8,128)(2,1)} fusion(bf16[6,16,72,512]{3,2,1,0:T(8,128)(2,1)} %get-tuple-element.121, s32[]{:T(128)} %get-tuple-element.120, bf16[16,200,512]{2,0,1:T(8,128)(2,1)S(1)} %convolution_convert_fusion.4, f32[16,512]{1,0:T(8,128)S(1)} %fusion.94, bf16[6,16,200,72]{2,3,1,0:T(8,128)(2,1)} %get-tuple-element.129), kind=kOutput, calls=%fused_computation.5.clone.1 | convolution fusion | flops 237109248 | bytes 5080064 | tf_op jit(solution)/shard_map/while/body/eval_jaxpr/lqd,lqt->ldt/dot_general | solution.py:50
  185.3 2.9 convolution_convert_fusion.4
  188.4 5.8 %fusion.95 = bf16[6,16,72,512]{3,2,1,0:T(8,128)(2,1)} fusion(bf16[6,16,72,512]{3,2,1,0:T(8,128)(2,1)} %get-tuple-element.121, s32[]{:T(128)} %get-tuple-element.120, bf16[16,200,512]{2,0,1:T(8,128)(2,1)S(1)} %convolution_convert_fusion.4, f32[16,512]{1,0:T(8,128)S(1)} %fusion.94, bf16[6,16,200,72]{2,3,1,0:T(8,128)(2,1)} %get-tuple-element.129), kind=kOutput, calls=%fused_computation.5.clone.1 | convolution fusion | flops 237109248 | bytes 5080064 | tf_op jit(solution)/shard_map/while/body/eval_jaxpr/lqd,lqt->ldt/dot_general | solution.py:50
  194.2 2.9 convolution_convert_fusion.4
  197.2 5.8 %fusion.95 = bf16[6,16,72,512]{3,2,1,0:T(8,128)(2,1)} fusion(bf16[6,16,72,512]{3,2,1,0:T(8,128)(2,1)} %get-tuple-element.121, s32[]{:T(128)} %get-tuple-element.120, bf16[16,200,512]{2,0,1:T(8,128)(2,1)S(1)} %convolution_convert_fusion.4, f32[16,512]{1,0:T(8,128)S(1)} %fusion.94, bf16[6,16,200,72]{2,3,1,0:T(8,128)(2,1)} %get-tuple-element.129), kind=kOutput, calls=%fused_computation.5.clone.1 | convolution fusion | flops 237109248 | bytes 5080064 | tf_op jit(solution)/shard_map/while/body/eval_jaxpr/lqd,lqt->ldt/dot_general | solution.py:50
  203.1 2.9 convolution_convert_fusion.4
  206.1 5.9 %fusion.95 = bf16[6,16,72,512]{3,2,1,0:T(8,128)(2,1)} fusion(bf16[6,16,72,512]{3,2,1,0:T(8,128)(2,1)} %get-tuple-element.121, s32[]{:T(128)} %get-tuple-element.120, bf16[16,200,512]{2,0,1:T(8,128)(2,1)S(1)} %convolution_convert_fusion.4, f32[16,512]{1,0:T(8,128)S(1)} %fusion.94, bf16[6,16,200,72]{2,3,1,0:T(8,128)(2,1)} %get-tuple-element.129), kind=kOutput, calls=%fused_computation.5.clone.1 | convolution fusion | flops 237109248 | bytes 5080064 | tf_op jit(solution)/shard_map/while/body/eval_jaxpr/lqd,lqt->ldt/dot_general | solution.py:50
  212.0 2.9 convolution_convert_fusion.4
  215.0 5.8 %fusion.95 = bf16[6,16,72,512]{3,2,1,0:T(8,128)(2,1)} fusion(bf16[6,16,72,512]{3,2,1,0:T(8,128)(2,1)} %get-tuple-element.121, s32[]{:T(128)} %get-tuple-element.120, bf16[16,200,512]{2,0,1:T(8,128)(2,1)S(1)} %convolution_convert_fusion.4, f32[16,512]{1,0:T(8,128)S(1)} %fusion.94, bf16[6,16,200,72]{2,3,1,0:T(8,128)(2,1)} %get-tuple-element.129), kind=kOutput, calls=%fused_computation.5.clone.1 | convolution fusion | flops 237109248 | bytes 5080064 | tf_op jit(solution)/shard_map/while/body/eval_jaxpr/lqd,lqt->ldt/dot_general | solution.py:50
  220.9 5.1 %fusion.21 = f32[14,72,512]{2,0,1:T(8,128)S(1)} fusion(bf16[96,72,512]{2,1,0:T(8,128)(2,1)} %bitcast.106, s32[96]{0:T(128)S(1)} %fusion.63, pred[96]{0:T(512)(128)(4,1)S(1)} %lt.59), kind=kOutput, calls=%fused_computation.17 | convolution fusion | flops 99093120 | bytes 9142752 | tf_op jit(solution)/shard_map/ls,spe->lpe/dot_general | solution.py:131
  227.9 1.2 convolution_convert_fusion.2
  229.1 3.8 %reshape.150 = bf16[13,72,2,8,64]{4,3,2,1,0:T(8,128)(2,1)} reshape(bf16[936,1024]{1,0:T(8,128)(2,1)S(1)} %convolution_convert_fusion.2) | data formatting | bytes 3833856 | tf_op jit(solution)/shard_map/reshape | solution.py:65
  232.9 3.6 %fusion.65 = (bf16[13,72,1,8,64]{4,3,2,1,0:T(8,128)(2,1)}, bf16[13,72,1,8,64]{4,3,2,1,0:T(8,128)(2,1)S(1)}) fusion(bf16[13,72,2,8,64]{4,3,2,1,0:T(8,128)(2,1)} %reshape.150), kind=kLoop, calls=%fused_computation.85 | loop fusion | bytes 3833856 | tf_op jit(solution)/shard_map/slice | solution.py:74
  236.5 3.2 %copy.106 = bf16[13,72,1,8,64]{1,4,0,3,2:T(8,128)(2,1)} copy(bf16[13,72,1,8,64]{4,3,2,1,0:T(8,128)(2,1)S(1)} %get-tuple-element.68) | data formatting | bytes 1916928
  239.7 2.0 fusion.67
  242.5 2.7 copy.81
  245.1 2.4 fusion.36
  247.9 1.3 convolution_add_fusion.1
  249.4 1.4 slice_add_fusion.1
  252.0 1.5 collective-permute-start.1
  254.2 9.3 %collective-permute-done = bf16[4,6,12,512]{3,2,1,0:T(8,128)(2,1)S(1)} collective-permute-done((bf16[4,6,12,512]{3,2,1,0:T(8,128)(2,1)S(1)}, bf16[4,6,12,512]{3,2,1,0:T(8,128)(2,1)S(1)}, u32[]{:S(2)}, u32[]{:S(2)}) %collective-permute-start) | collective-permute-done | bytes 294944 | tf_op jit(solution)/shard_map/ppermute | solution.py:21
  264.7 1.0 reshape.152
  265.7 1.2 copy.85
  267.9 3.4 %convolution_convert_fusion.1 = bf16[576,1536]{1,0:T(8,128)(2,1)} fusion(bf16[576,512]{1,0:T(8,128)(2,1)} %reshape.153, bf16[512,1536]{1,0:T(8,128)(2,1)S(1)} %copy-done), kind=kOutput, calls=%fused_computation.23 | convolution fusion | flops 906854400 | bytes 3932160 | tf_op jit(solution)/shard_map/dot_general | solution.py:153
  271.3 5.6 %reshape.188 = bf16[4,144,3,8,64]{4,3,2,1,0:T(8,128)(2,1)} reshape(bf16[576,1536]{1,0:T(8,128)(2,1)} %convolution_convert_fusion.1) | data formatting | bytes 3538944 | tf_op jit(solution)/shard_map/reshape;reshape | solution.py:87
  276.8 3.6 %fusion.66 = (bf16[4,144,1,8,64]{4,3,2,1,0:T(8,128)(2,1)S(1)}, bf16[4,144,1,8,64]{4,3,2,1,0:T(8,128)(2,1)}, bf16[4,144,1,8,64]{4,3,2,1,0:T(8,128)(2,1)}) fusion(bf16[4,144,3,8,64]{4,3,2,1,0:T(8,128)(2,1)} %reshape.188), kind=kLoop, calls=%fused_computation.86 | loop fusion | bytes 3538944 | tf_op jit(solution)/shard_map/slice | solution.py:93
  280.5 2.6 copy.108
  283.0 2.6 copy.109
  285.6 2.4 fusion.44
  288.0 3.9 %fusion.68 = (f32[4,8,144]{2,1,0:T(8,128)}, f32[4,8,144,144]{2,3,1,0:T(8,128)}) fusion(f32[4,8,144,144]{2,3,1,0:T(8,128)S(1)} %fusion.44), kind=kOutput, calls=%fused_computation.88 | output fusion | flops 2654351 | bytes 5326848 | tf_op jit(solution)/shard_map/sub | solution.py:91
  292.0 1.6 copy.107
  293.6 4.1 %fusion.33 = bf16[4,144,8,64]{1,3,2,0:T(8,128)(2,1)} fusion(f32[4,8,144,144]{2,3,1,0:T(8,128)} %get-tuple-element.75, f32[4,8,144]{2,1,0:T(8,128)} %get-tuple-element.74, bf16[4,144,1,8,64]{1,4,3,0,2:T(8,128)(2,1)} %copy.107), kind=kOutput, calls=%fused_computation.34 | convolution fusion | flops 86556672 | bytes 3852288 | tf_op jit(solution)/shard_map/whqk,wkhd->wqhd/dot_general | solution.py:92
  297.7 2.1 copy.91
  299.8 1.4 reshape_reshape.7
  301.2 1.2 copy.101
  303.4 1.6 fusion.37
  305.0 0.9 copy.94
  (71 shorter events, 10.7 us)
Async XLA Ops:
  0.0 267.9 %copy-start = (bf16[512,1536]{1,0:T(8,128)(2,1)S(1)}, bf16[512,1536]{1,0:T(8,128)(2,1)}, u32[]{:S(2)}) copy-start(bf16[512,1536]{1,0:T(8,128)(2,1)} %param.27) | copy-start | bytes 4718596
  6.8 7.3 %copy-start.8 = (s32[1,6]{1,0:T(1,128)S(1)}, s32[1,6]{1,0:T(1,128)}, u32[]{:S(2)}) copy-start(s32[1,6]{1,0:T(1,128)} %param.17) | copy-start | bytes 76
  6.8 135.3 %copy-start.5 = (bf16[14,512]{1,0:T(8,128)(2,1)S(1)}, bf16[14,512]{1,0:T(8,128)(2,1)}, u32[]{:S(2)}) copy-start(bf16[14,512]{1,0:T(8,128)(2,1)} %param.21) | copy-start | bytes 43012
  6.8 135.6 %copy-start.3 = (bf16[9,200,512]{2,1,0:T(8,128)(2,1)S(1)}, bf16[9,200,512]{2,1,0:T(8,128)(2,1)}, u32[]{:S(2)}) copy-start(bf16[9,200,512]{2,1,0:T(8,128)(2,1)} %param.19) | copy-start | bytes 5529604
  6.8 155.7 %all-to-all-start = ((bf16[6,200,1152]{1,0,2:T(8,128)(2,1)}), bf16[6,200,1152]{1,0,2:T(8,128)(2,1)}, u32[]{:S(2)}, u32[]{:S(2)}) async-start(bf16[6,200,1152]{1,0,2:T(8,128)(2,1)} %copy.72), calls=%async_computation | async-start | bytes 9437184 | tf_op jit(solution)/shard_map/all_to_all | solution.py:124
  14.1 131.7 %copy-start.10 = (u32[32]{0:T(128)S(1)}, u32[32]{0:T(128)}, u32[]{:S(2)}) copy-start(u32[32]{0:T(128)} %constant.68) | copy-start | bytes 388
  14.1 146.9 %copy-start.6 = (bf16[3,512]{1,0:T(4,128)(2,1)S(1)}, bf16[3,512]{1,0:T(4,128)(2,1)}, u32[]{:S(2)}) copy-start(bf16[3,512]{1,0:T(4,128)(2,1)} %param.22) | copy-start | bytes 9220
  142.5 19.9 %copy-start.7 = (bf16[512]{0:T(512)(128)(2,1)S(1)}, bf16[512]{0:T(512)(128)(2,1)}, u32[]{:S(2)}) copy-start(bf16[512]{0:T(512)(128)(2,1)} %param.26) | copy-start | bytes 3076
  162.5 5.0 %copy-start.4 = (bf16[9,512]{1,0:T(8,128)(2,1)S(1)}, bf16[9,512]{1,0:T(8,128)(2,1)}, u32[]{:S(2)}) copy-start(bf16[9,512]{1,0:T(8,128)(2,1)} %param.20) | copy-start | bytes 27652
  225.9 1.4 copy-start.1
  225.9 2.0 copy-start.9
  239.7 5.4 %copy-start.2 = (bf16[13,72,1,8,64]{4,3,2,1,0:T(8,128)(2,1)S(1)}, bf16[13,72,1,8,64]{4,3,2,1,0:T(8,128)(2,1)}, u32[]{:S(2)}) copy-start(bf16[13,72,1,8,64]{4,3,2,1,0:T(8,128)(2,1)} %get-tuple-element.67) | copy-start | bytes 2875396
  251.4 12.0 %collective-permute-start = (bf16[4,6,12,512]{3,2,1,0:T(8,128)(2,1)S(1)}, bf16[4,6,12,512]{3,2,1,0:T(8,128)(2,1)S(1)}, u32[]{:S(2)}, u32[]{:S(2)}) collective-permute-start(bf16[4,6,12,512]{3,2,1,0:T(8,128)(2,1)S(1)} %multiply_convert_fusion), channel_id=1, source_target_pairs={{28,0},{30,2},{0,4},{2,6},{4,8},{6,10},{8,12},{10,14},{12,16},{14,... | collective-permute-start | bytes 884744 | tf_op jit(solution)/shard_map/ppermute | solution.py:21
  252.0 11.4 %collective-permute-start.1 = (bf16[4,6,12,512]{3,2,1,0:T(8,128)(2,1)S(1)}, bf16[4,6,12,512]{3,2,1,0:T(8,128)(2,1)S(1)}, u32[]{:S(2)}, u32[]{:S(2)}) collective-permute-start(bf16[4,6,12,512]{3,2,1,0:T(8,128)(2,1)S(1)} %multiply_convert_fusion), channel_id=1, source_target_pairs={{4,0},{6,2},{8,4},{10,6},{12,8},{14,10},{16,12},{18,14},{20,16},{2... | collective-permute-start | bytes 884744 | tf_op jit(solution)/shard_map/ppermute | solution.py:21
where the time goes:
time: 309 us; the launch traced here: 306 us
  blocking collectives  141 us (46%)
  matrix products  77.9 us (25%)
  local copies, waits for them, and re-layouts  58.1 us (19%)
  starting transfers between devices  9.39 us (3%)
  waiting for transfers between devices  9.31 us (3%)
  other arithmetic  8.22 us (3%)
    all_gather x1, blocking collectives, local(): lax.all_gather(channel_index_table, 'tile', axis=0, tiled=True)  128 us
    dot_general x6, matrix products, one_block(): jnp.einsum('lqd,lqt->ldt', unprocessed_part, chosen_weight, preferred_ele...  35.1 us
    unnamed x31, local copies, waits for them, and re-layouts  19.2 us
    dot_general x6, matrix products, one_block(): jnp.einsum('lk,kqt->lqt', pick_piece, patch_weight, preferred_element_typ...  17.4 us
    unnamed x1, blocking collectives  13.7 us
    ppermute x2, waiting for transfers between devices, passed_along(): return lax.ppermute(block, axis, route)  9.31 us
    all_to_all x1, starting transfers between devices, local(): lax.all_to_all(pixels, 'tile', split_axis=2, concat_axis=0, tiled=True)  7.31 us
  transfers between devices with their start and end apart: 3, of which 1 were waited for; matrix products, arithmetic and copies ran while one was open for 2% of the time, Pallas kernels for 0%

commit v1 on v0

v1 whole, which is shorter than its diff:
```python
import functools
import math

import jax
import jax.numpy as jnp
from jax import lax
from jax.experimental import pallas as pl
from jax.experimental.pallas import tpu as pltpu
from jax.sharding import PartitionSpec as P

LEVELS = 13
V_ATM = 5
V_SURF = 4
LATENT = 3
HEADS = 8
WL = 2
WH = 6
WW = 12
LT = 8
CHANNELS = V_ATM * LEVELS + V_SURF
F32 = jnp.float32
BF16 = jnp.bfloat16
NT = (((1,), (1,)), ((), ()))


def exchange_and_perceive(
    n, cap, kinds, slot_of, x_ref, weight, bias, code, latents, perc_query, perc_kv,
    perc_out, gain, state_ref, normed_ref, recv, emb, pair, logits, gath, send_sem, recv_sem,
):
    me = lax.axis_index("tile")
    member = lax.axis_index("member")
    patches, packed = x_ref.shape[1:]
    pix = packed // cap
    width = weight.shape[2]
    head = width // HEADS

    barrier = pltpu.get_barrier_semaphore()

    def greet(k, carry):
        pl.semaphore_signal(barrier, inc=1, device_id={"tile": lax.rem(me + k, n)})
        return carry

    lax.fori_loop(1, n, greet, 0)
    pl.semaphore_wait(barrier, n - 1)

    def offset(i):
        half = n // 2
        step = (i + 1) // 2
        return half + step - 2 * step * (i % 2)

    def copy(k):
        to = lax.rem(me + k, n)
        return pltpu.make_async_remote_copy(
            src_ref=x_ref.at[to],
            dst_ref=recv.at[me],
            send_sem=send_sem.at[k],
            recv_sem=recv_sem.at[k],
            device_id={"tile": to},
        )

    def launch(i, carry):
        copy(offset(i)).start()
        return carry

    lax.fori_loop(0, n - 1, launch, 0)

    def embed(block, source):
        for s in range(cap):
            slot = source * cap + s
            kind = kinds[slot]
            value = jnp.dot(
                block[:, s * pix:(s + 1) * pix], weight[kind], preferred_element_type=F32
            )
            emb[slot] = (value + bias[kind].astype(F32)).astype(BF16)

    embed(x_ref[me], me)

    query = jnp.dot(latents[...], perc_query[...], preferred_element_type=F32) / math.sqrt(head)
    lane_head = lax.broadcasted_iota(jnp.int32, (HEADS, width), 1) // head
    row_head = lax.broadcasted_iota(jnp.int32, (HEADS, width), 0)
    own_head = lane_head == row_head
    spread = [jnp.where(own_head, query[j:j + 1, :], 0.0) for j in range(LATENT)]
    spread.append(jnp.zeros((HEADS, width), F32))
    rows = jnp.concatenate(spread, axis=0)
    rows_high = rows.astype(BF16)
    rows_low = (rows - rows_high.astype(F32)).astype(BF16)

    def land(i, carry):
        k = offset(i)
        copy(k).wait_recv()
        source = lax.rem(me + n - k, n)
        embed(recv[source], source)
        return carry

    lax.fori_loop(0, n - 1, land, 0)

    def one_level(l, carry):
        total = emb[slot_of[l]].astype(F32)
        for v in range(1, V_ATM):
            total = total + emb[slot_of[v * LEVELS + l]].astype(F32)
        token = (total + code[l].astype(F32)).astype(BF16)
        both = jnp.dot(token, perc_kv[...], preferred_element_type=F32).astype(BF16)
        pair[l] = both[:, width:]
        keys = both[:, :width]
        logits[l] = lax.dot_general(
            keys, rows_high, NT, preferred_element_type=F32
        ) + lax.dot_general(keys, rows_low, NT, preferred_element_type=F32)
        return carry

    lax.fori_loop(0, LEVELS, one_level, 0)

    top = logits[0]
    for l in range(1, LEVELS):
        top = jnp.maximum(top, logits[l])
    norm = jnp.zeros_like(top)
    for l in range(LEVELS):
        power = jnp.exp(logits[l] - top)
        logits[l] = power
        norm = norm + power
    scale = 1.0 / norm

    wide_row = lax.broadcasted_iota(jnp.int32, (4 * HEADS, LATENT * width), 0)
    wide_lane = lax.broadcasted_iota(jnp.int32, (4 * HEADS, LATENT * width), 1) // head
    expand = jnp.where(wide_row == wide_lane, 1.0, 0.0).astype(BF16)
    gath[...] = jnp.zeros_like(gath)

    def weigh(l, carry):
        attn = (logits[l] * scale).astype(BF16)
        value = pair[l].astype(F32)
        wide = jnp.dot(attn, expand, preferred_element_type=F32)
        for j in range(LATENT):
            gath[j] += wide[:, j * width:(j + 1) * width] * value
        return carry

    lax.fori_loop(0, LEVELS, weigh, 0)

    surface = emb[slot_of[V_ATM * LEVELS]].astype(F32)
    for c in range(V_ATM * LEVELS + 1, CHANNELS):
        surface = surface + emb[slot_of[c]].astype(F32)
    surface = surface + code[LEVELS].astype(F32)
    for j in range(LATENT + 1):
        if j < LATENT:
            state = latents[j:j + 1, :].astype(F32) + jnp.dot(
                gath[j].astype(BF16), perc_out[...], preferred_element_type=F32
            )
        else:
            state = surface
        center = state - jnp.mean(state, axis=-1, keepdims=True)
        spread_of = jnp.mean(center * center, axis=-1, keepdims=True)
        state_ref[j] = state
        normed_ref[j] = (
            center * lax.rsqrt(spread_of + 1e-05) * gain[...].astype(F32)
        ).astype(BF16)

    def drain(i, carry):
        copy(offset(i)).wait_send()
        return carry

    lax.fori_loop(0, n - 1, drain, 0)


def window_attention(
    shift_ref, state_ref, own_ref, left_ref, right_ref, qkv_ref, out_w_ref, out_ref,
    own_triple, near_pair, mixed_ref,
):
    levels, patches, width = own_ref.shape
    head = width // HEADS
    members = WL * patches
    offset = shift_ref[0]
    rows = levels * patches
    column = lax.broadcasted_iota(jnp.int32, (levels, patches, width), 1) % WW
    near = jnp.where(
        column >= offset, left_ref[...].astype(F32), right_ref[...].astype(F32)
    ).astype(BF16)
    own_triple[...] = jnp.dot(
        own_ref[...].reshape(rows, width), qkv_ref[...], preferred_element_type=F32
    ).astype(BF16)
    near_pair[...] = jnp.dot(
        near.reshape(rows, width), qkv_ref[:, width:], preferred_element_type=F32
    ).astype(BF16)
    q_first = lax.broadcasted_iota(jnp.int32, (members, members), 0) % WW < offset
    k_first = lax.broadcasted_iota(jnp.int32, (members, members), 1) % WW < offset
    same = q_first == k_first
    lane = lax.broadcasted_iota(jnp.int32, (members, 2 * head), 1) // head
    scale = 1.0 / math.sqrt(head)
    for g in range(levels // WL):
        r = slice(g * members, (g + 1) * members)
        for h2 in range(HEADS // 2):
            c = slice(h2 * 2 * head, (h2 + 1) * 2 * head)
            ck = slice(width + h2 * 2 * head, width + (h2 + 1) * 2 * head)
            cv = slice(2 * width + h2 * 2 * head, 2 * width + (h2 + 1) * 2 * head)
            q = own_triple[r, c]
            k_own = own_triple[r, ck]
            v_own = own_triple[r, cv]
            k_near = near_pair[r, c]
            v_near = near_pair[r, ck]
            halves = []
            for one in range(2):
                q_one = jnp.where(lane == one, q, jnp.zeros_like(q))
                a = lax.dot_general(q_one, k_own, NT, preferred_element_type=F32) * scale
                b = lax.dot_general(q_one, k_near, NT, preferred_element_type=F32) * scale
                a = jnp.where(same, a, -jnp.inf)
                b = jnp.where(same, -jnp.inf, b)
                top = jnp.maximum(
                    jnp.max(a, axis=-1, keepdims=True), jnp.max(b, axis=-1, keepdims=True)
                )
                a = jnp.exp(a - top)
                b = jnp.exp(b - top)
                norm = 1.0 / (
                    jnp.sum(a, axis=-1, keepdims=True) + jnp.sum(b, axis=-1, keepdims=True)
                )
                halves.append(
                    jnp.dot((a * norm).astype(BF16), v_own, preferred_element_type=F32)
                    + jnp.dot((b * norm).astype(BF16), v_near, preferred_element_type=F32)
                )
            mixed_ref[r, c] = jnp.where(lane == 0, halves[0], halves[1]).astype(BF16)
    result = state_ref[...].reshape(rows, width) + jnp.dot(
        mixed_ref[...], out_w_ref[...], preferred_element_type=F32
    )
    for i in range(levels * WH):
        out_ref[i // WH, 0, i % WH] = result[i * WW:(i + 1) * WW, :].astype(BF16)


def passed_along(block, axis, distance):
    devices = range(lax.axis_size(axis))
    route = [((i - distance) % len(devices), i) for i in devices]
    return lax.ppermute(block, axis, route)


def local(
    pixels, channel_index_table, group_sizes, patch_weight, patch_bias, level_code, latents,
    perc_query, perc_kv, perc_out, norm_gain, window_qkv, window_out, shift,
):
    n = lax.axis_size("tile")
    bands = n // LT
    cap, pix, all_patches = pixels.shape
    patches = all_patches // n
    kind_count, _, width = patch_weight.shape
    vmem = pl.BlockSpec(memory_space=pltpu.VMEM)
    smem = pl.BlockSpec(memory_space=pltpu.SMEM)

    slot = jnp.arange(cap, dtype=jnp.int32)[None, :]
    marked = jnp.where(
        slot < group_sizes[:, None], channel_index_table, channel_index_table + CHANNELS
    )
    marked = lax.all_gather(marked, "tile", axis=0, tiled=True).reshape(-1)
    slot_of = jnp.argmax(
        marked[None, :] == jnp.arange(CHANNELS, dtype=jnp.int32)[:, None], axis=1
    ).astype(jnp.int32)
    ids = marked % CHANNELS
    kinds = jnp.where(ids < V_ATM * LEVELS, ids // LEVELS, ids - V_ATM * LEVELS + V_ATM)

    blocks = pixels.reshape(cap * pix, all_patches).T.reshape(n, patches, cap * pix)
    state, normed = pl.pallas_call(
        functools.partial(exchange_and_perceive, n, cap),
        out_shape=(
            jax.ShapeDtypeStruct((LATENT + 1, patches, width), F32),
            jax.ShapeDtypeStruct((LATENT + 1, patches, width), BF16),
        ),
        in_specs=[smem, smem] + [vmem] * 9,
        out_specs=(vmem, vmem),
        scratch_shapes=[
            pltpu.VMEM((n, patches, cap * pix), BF16),
            pltpu.VMEM((n * cap, patches, width), BF16),
            pltpu.VMEM((LEVELS, patches, width), BF16),
            pltpu.VMEM((LEVELS, patches, 4 * HEADS), F32),
            pltpu.VMEM((LATENT, patches, width), F32),
            pltpu.SemaphoreType.DMA((n,)),
            pltpu.SemaphoreType.DMA((n,)),
        ],
        compiler_params=pltpu.CompilerParams(
            collective_id=0, has_side_effects=True, vmem_limit_bytes=60 * 1024 * 1024
        ),
    )(
        kinds, slot_of, blocks, patch_weight, patch_bias.reshape(kind_count, 1, width),
        level_code.reshape(LEVELS + 1, 1, width), latents, perc_query, perc_kv, perc_out,
        norm_gain.reshape(1, width),
    )
    left = passed_along(normed, "tile", bands)
    right = passed_along(normed, "tile", -bands)
    return pl.pallas_call(
        window_attention,
        out_shape=jax.ShapeDtypeStruct((LATENT + 1, 1, WH, patches // WH, width), BF16),
        in_specs=[smem] + [vmem] * 6,
        out_specs=vmem,
        scratch_shapes=[
            pltpu.VMEM(((LATENT + 1) * patches, 3 * width), BF16),
            pltpu.VMEM(((LATENT + 1) * patches, 2 * width), BF16),
            pltpu.VMEM(((LATENT + 1) * patches, width), BF16),
        ],
        compiler_params=pltpu.CompilerParams(vmem_limit_bytes=60 * 1024 * 1024),
    )(shift, state, normed, left, right, window_qkv, window_out)


def solution(mesh):
    in_specs = (P("tile", "member", None), P("tile", None), P("tile")) + (P(),) * 11
    out_specs = P(None, "tile", "member", None, None)
    return jax.shard_map(local, mesh=mesh, in_specs=in_specs, out_specs=out_specs, check_vma=False)
```

time: 309 us -> 153 us (0.50)
  the two profiles are of different devices: /device:TPU:12 before, /device:TPU:16 now
where the time goes in v1:
time: 153 us
  Pallas kernels  93.8 us (61%)
  blocking collectives  30.6 us (20%)
  waiting for transfers between devices  11 us (7%)
  local copies, waits for them, and re-layouts  10.5 us (7%)
  starting transfers between devices  2.97 us (2%)
  other arithmetic  2.53 us (2%)
    pallas_call x1, Pallas kernels, local(): pl.pallas_call(functools.partial(exchange_and_perceive, n, cap), out_shap...  87.5 us
    all_gather x1, blocking collectives, local(): marked = lax.all_gather(marked, 'tile', axis=0, tiled=True).reshape(-1)  30.6 us
    ppermute x2, waiting for transfers between devices, passed_along(): return lax.ppermute(block, axis, route)  11 us
    pallas_call x1, Pallas kernels, local(): pl.pallas_call(window_attention, out_shape=jax.ShapeDtypeStruct((LATENT +...  6.28 us
    reshape x1, local copies, waits for them, and re-layouts, local(): pixels.reshape(cap * pix, all_patches).T.reshape(n, patches, cap * pix)  5.45 us
  transfers between devices with their start and end apart: 2, of which 2 were waited for; matrix products, arithmetic and copies ran while one was open for 0% of the time, Pallas kernels for 0%

profile of v1, /device:TPU:16, one launch (start us, length us, event | category | flops | bytes accessed | tf_op | source)
XLA Modules:
  0.0 152.7 jit_solution(14893210433071211995)
XLA Ops:
  0.7 0.7 fusion
  1.3 30.6 %all-gather = s32[16,1,6]{2,1,0:T(1,128)S(1)} all-gather(s32[1,1,6]{2,1,0:T(1,128)S(1)} %fusion), channel_id=1, replica_groups=mesh['tile'=16,'member'=2] {'tile'}, dimensions={0}, use_global_device_ids=true | all-gather | bytes 408 | tf_op jit(solution)/shard_map/all_gather | solution.py:246
  31.9 0.5 broadcast.27
  32.4 0.7 reduce.22
  33.1 0.1 reshape.30
  33.2 0.7 iota_reduce_fusion
  33.9 0.5 compare_select_fusion.kinds
  34.4 0.0 copy-start.3
  34.4 0.0 copy-start.2
  34.4 0.0 copy-start.4
  34.4 5.5 %copy.25 = bf16[1200,1152]{0,1:T(8,128)(2,1)} copy(bf16[1200,1152]{1,0:T(8,128)(2,1)} %bitcast.11) | data formatting | bytes 5529600 | tf_op jit(solution)/shard_map/reshape | solution.py:253
  39.9 0.0 copy-done.3
  39.9 0.6 copy.27.code
  40.5 0.0 copy-done.2
  40.5 0.6 copy.26.bias
  41.1 0.0 copy-done.4
  41.1 0.6 reshape.35.gain
  41.7 87.5 %shard_map.136 = (f32[4,72,512]{2,1,0:T(8,128)}, bf16[4,72,512]{2,1,0:T(8,128)(2,1)}) custom-call(s32[96]{0:T(128)} %compare_select_fusion.kinds, s32[69]{0:T(128)} %get-tuple-element.8.slot_of, bf16[16,72,1200]{2,1,0:T(8,128)(2,1)} %bitcast.10, bf16[9,200,512]{2,1,0:T(8,128)(2,1)} %weight.1, bf16[9,1,512]{2,1,0:T(2,128)(2,1)} %copy.26.bias, ...), custom_call_target="tpu_custom_call" | custom-call | tf_op jit(solution)/shard_map/pallas_call | solution.py:254
  129.2 0.1 collective-permute-start
  129.3 2.9 %collective-permute-start.1 = (bf16[4,72,512]{2,1,0:T(8,128)(2,1)}, bf16[4,72,512]{2,1,0:T(8,128)(2,1)S(1)}, u32[]{:S(2)}, u32[]{:S(2)}) collective-permute-start(bf16[4,72,512]{2,1,0:T(8,128)(2,1)} %get-tuple-element.10.own_ref), channel_id=1, source_target_pairs={{4,0},{6,2},{8,4},{10,6},{12,8},{14,10},{16,12},{18,14},{20,16},{2... | collective-permute-start | bytes 884744 | tf_op jit(solution)/shard_map/ppermute | solution.py:227
  132.8 5.6 %collective-permute-done.left_ref = bf16[4,72,512]{2,1,0:T(8,128)(2,1)S(1)} collective-permute-done((bf16[4,72,512]{2,1,0:T(8,128)(2,1)}, bf16[4,72,512]{2,1,0:T(8,128)(2,1)S(1)}, u32[]{:S(2)}, u32[]{:S(2)}) %collective-permute-start) | collective-permute-done | bytes 294944 | tf_op jit(solution)/shard_map/ppermute | solution.py:227
  138.4 0.0 copy-start
  138.4 5.4 %collective-permute-done.1.right_ref = bf16[4,72,512]{2,1,0:T(8,128)(2,1)S(1)} collective-permute-done((bf16[4,72,512]{2,1,0:T(8,128)(2,1)}, bf16[4,72,512]{2,1,0:T(8,128)(2,1)S(1)}, u32[]{:S(2)}, u32[]{:S(2)}) %collective-permute-start.1) | collective-permute-done | bytes 294944 | tf_op jit(solution)/shard_map/ppermute | solution.py:227
  143.8 0.0 copy-start.1
  143.8 0.0 copy-done
  143.8 0.7 copy-done.1
  144.5 6.3 %shard_map.137 = bf16[4,1,6,12,512]{4,3,2,1,0:T(8,128)(2,1)} custom-call(s32[1]{0:T(128)S(6)} %copy.30.shift_ref, f32[4,72,512]{2,1,0:T(8,128)} %get-tuple-element.9.state_ref, bf16[4,72,512]{2,1,0:T(8,128)(2,1)} %get-tuple-element.10.own_ref, bf16[4,72,512]{2,1,0:T(8,128)(2,1)} %copy-done, bf16[4,72,512]{2,1,0:T(8,128)(2,1)} %copy-done.1, ...), custom_call_target="tpu_custom_call" | custom-call | tf_op jit(solution)/shard_map/pallas_call | solution.py:281
  150.8 1.9 %copy.28 = bf16[4,1,6,12,512]{4,0,3,2,1:T(4,128)(2,1)} copy(bf16[4,1,6,12,512]{4,3,2,1,0:T(8,128)(2,1)} %shard_map.137) | data formatting | bytes 589824 | tf_op jit(solution)/shard_map/pallas_call | solution.py:281
Async XLA Ops:
  34.4 5.5 %copy-start.3 = (bf16[14,512]{1,0:T(8,128)(2,1)S(1)}, bf16[14,512]{1,0:T(8,128)(2,1)}, u32[]{:S(2)}) copy-start(bf16[14,512]{1,0:T(8,128)(2,1)} %param.19) | copy-start | bytes 43012
  34.4 6.1 %copy-start.2 = (bf16[9,512]{1,0:T(8,128)(2,1)S(1)}, bf16[9,512]{1,0:T(8,128)(2,1)}, u32[]{:S(2)}) copy-start(bf16[9,512]{1,0:T(8,128)(2,1)} %param.18) | copy-start | bytes 27652
  34.4 6.7 %copy-start.4 = (bf16[512]{0:T(512)(128)(2,1)S(1)}, bf16[512]{0:T(512)(128)(2,1)}, u32[]{:S(2)}) copy-start(bf16[512]{0:T(512)(128)(2,1)} %param.24) | copy-start | bytes 3076
  129.2 9.2 %collective-permute-start = (bf16[4,72,512]{2,1,0:T(8,128)(2,1)}, bf16[4,72,512]{2,1,0:T(8,128)(2,1)S(1)}, u32[]{:S(2)}, u32[]{:S(2)}) collective-permute-start(bf16[4,72,512]{2,1,0:T(8,128)(2,1)} %get-tuple-element.10.own_ref), channel_id=1, source_target_pairs={{28,0},{30,2},{0,4},{2,6},{4,8},{6,10},{8,12},{10,14},{12,16},{14,... | collective-permute-start | bytes 884744 | tf_op jit(solution)/shard_map/ppermute | solution.py:227
  129.3 14.5 %collective-permute-start.1 = (bf16[4,72,512]{2,1,0:T(8,128)(2,1)}, bf16[4,72,512]{2,1,0:T(8,128)(2,1)S(1)}, u32[]{:S(2)}, u32[]{:S(2)}) collective-permute-start(bf16[4,72,512]{2,1,0:T(8,128)(2,1)} %get-tuple-element.10.own_ref), channel_id=1, source_target_pairs={{4,0},{6,2},{8,4},{10,6},{12,8},{14,10},{16,12},{18,14},{20,16},{2... | collective-permute-start | bytes 884744 | tf_op jit(solution)/shard_map/ppermute | solution.py:227
  138.4 5.4 %copy-start = (bf16[4,72,512]{2,1,0:T(8,128)(2,1)}, bf16[4,72,512]{2,1,0:T(8,128)(2,1)S(1)}, u32[]{:S(2)}) copy-start(bf16[4,72,512]{2,1,0:T(8,128)(2,1)S(1)} %collective-permute-done.left_ref) | copy-start | bytes 884740
  143.8 0.7 copy-start.1

commit v2 on v1

v2 whole, which is shorter than its diff:
```python
import functools
import math

import jax
import jax.numpy as jnp
from jax import lax
from jax.experimental import pallas as pl
from jax.experimental.pallas import tpu as pltpu
from jax.sharding import PartitionSpec as P

LEVELS = 13
V_ATM = 5
V_SURF = 4
LATENT = 3
HEADS = 8
WL = 2
WH = 6
WW = 12
LT = 8
CHANNELS = V_ATM * LEVELS + V_SURF
F32 = jnp.float32
BF16 = jnp.bfloat16
NT = (((1,), (1,)), ((), ()))


def encode(
    n, cap, shift_ref, marked_ref, x_ref, weight, bias, code, latents, perc_query, perc_kv,
    perc_out, gain, qkv_ref, out_w_ref, out_ref, recv, emb, pair, logits, gath, recv_ids,
    inverse, ids, slot_of, bias_rows, code_rows, state_ref, normed_ref, left_ref, right_ref,
    own_triple, near_pair, mixed_ref, send_sem, recv_sem, table_send, table_recv, local_sem,
    rim_send, rim_recv,
):
    me = lax.axis_index("tile")
    bands = n // LT
    patches, packed = x_ref.shape[1:]
    pix = packed // cap
    width = weight.shape[2]
    head = width // HEADS

    barrier = pltpu.get_barrier_semaphore()

    def greet(k, carry):
        pl.semaphore_signal(barrier, inc=1, device_id={"tile": lax.rem(me + k, n)})
        return carry

    lax.fori_loop(1, n, greet, 0)
    pl.semaphore_wait(barrier, n - 1)

    def offset(i):
        half = n // 2
        step = (i + 1) // 2
        return half + step - 2 * step * (i % 2)

    def table_copy(k):
        return pltpu.make_async_remote_copy(
            src_ref=marked_ref,
            dst_ref=recv_ids.at[me],
            send_sem=table_send.at[k],
            recv_sem=table_recv.at[k],
            device_id={"tile": lax.rem(me + k, n)},
        )

    def copy(k):
        to = lax.rem(me + k, n)
        return pltpu.make_async_remote_copy(
            src_ref=x_ref.at[to],
            dst_ref=recv.at[me],
            send_sem=send_sem.at[k],
            recv_sem=recv_sem.at[k],
            device_id={"tile": to},
        )

    def launch(i, carry):
        table_copy(offset(i)).start()
        return carry

    lax.fori_loop(0, n - 1, launch, 0)

    def launch_block(i, carry):
        copy(offset(i)).start()
        return carry

    lax.fori_loop(0, n - 1, launch_block, 0)

    recv_ids[me] = marked_ref[...]
    for i in range(bias.shape[0]):
        bias_rows[i] = bias[i:i + 1, :].astype(F32)
    for i in range(code.shape[0]):
        code_rows[i] = code[i:i + 1, :].astype(F32)

    query = jnp.dot(latents[...], perc_query[...], preferred_element_type=F32) / math.sqrt(head)
    lane_head = lax.broadcasted_iota(jnp.int32, (HEADS, width), 1) // head
    row_head = lax.broadcasted_iota(jnp.int32, (HEADS, width), 0)
    own_head = lane_head == row_head
    spread = [jnp.where(own_head, query[j:j + 1, :], 0.0) for j in range(LATENT)]
    spread.append(jnp.zeros((HEADS, width), F32))
    rows = jnp.concatenate(spread, axis=0)
    rows_high = rows.astype(BF16)
    rows_low = (rows - rows_high.astype(F32)).astype(BF16)

    def table_land(k, carry):
        table_copy(k).wait_recv()
        return carry

    lax.fori_loop(1, n, table_land, 0)
    to_ids = pltpu.make_async_copy(recv_ids, ids, local_sem.at[0])
    to_ids.start()

    channel = lax.broadcasted_iota(jnp.int32, inverse.shape, 0)
    lane = lax.broadcasted_iota(jnp.int32, inverse.shape, 1)

    def match(d, found):
        hit = recv_ids[d] == channel
        return found + jnp.where(hit, (lane + d * cap).astype(F32), 0.0)

    found = lax.fori_loop(0, n, match, jnp.zeros(inverse.shape, F32))
    total = jnp.sum(found, axis=1, keepdims=True).astype(jnp.int32)
    inverse[...] = jnp.broadcast_to(total, inverse.shape)
    to_ids.wait()

    def embed(block, source):
        for s in range(cap):
            held = ids[source, 0, s]
            held = jnp.where(held >= CHANNELS, held - CHANNELS, held)
            kind = jnp.where(
                held < V_ATM * LEVELS, held // LEVELS, held - V_ATM * LEVELS + V_ATM
            )
            kind = jnp.clip(kind, 0, weight.shape[0] - 1)
            value = jnp.dot(
                block[:, s * pix:(s + 1) * pix], weight[kind], preferred_element_type=F32
            )
            emb[source * cap + s] = (value + bias_rows[kind]).astype(BF16)

    embed(x_ref[me], me)
    to_slots = pltpu.make_async_copy(inverse, slot_of, local_sem.at[1])
    to_slots.start()
    to_slots.wait()

    def land(i, carry):
        k = offset(i)
        copy(k).wait_recv()
        source = lax.rem(me + n - k, n)
        embed(recv[source], source)
        return carry

    lax.fori_loop(0, n - 1, land, 0)

    def channel_value(c):
        return emb[jnp.clip(slot_of[c, 0], 0, n * cap - 1)].astype(F32)

    def rim(j, side):
        to = lax.rem(me + bands, n) if side == 0 else lax.rem(me + n - bands, n)
        return pltpu.make_async_remote_copy(
            src_ref=normed_ref.at[j],
            dst_ref=(left_ref if side == 0 else right_ref).at[j],
            send_sem=rim_send.at[j, side],
            recv_sem=rim_recv.at[j, side],
            device_id={"tile": to},
        )

    def finish_level(j, state):
        center = state - jnp.mean(state, axis=-1, keepdims=True)
        spread_of = jnp.mean(center * center, axis=-1, keepdims=True)
        state_ref[j] = state
        normed_ref[j] = (
            center * lax.rsqrt(spread_of + 1e-05) * gain[...].astype(F32)
        ).astype(BF16)

    surface = channel_value(V_ATM * LEVELS)
    for c in range(V_ATM * LEVELS + 1, CHANNELS):
        surface = surface + channel_value(c)
    finish_level(LATENT, surface + code_rows[LEVELS])

    def one_level(l, carry):
        total = channel_value(l)
        for v in range(1, V_ATM):
            total = total + channel_value(v * LEVELS + l)
        token = (total + code_rows[l]).astype(BF16)
        both = jnp.dot(token, perc_kv[...], preferred_element_type=F32).astype(BF16)
        pair[l] = both[:, width:]
        keys = both[:, :width]
        logits[l] = lax.dot_general(
            keys, rows_high, NT, preferred_element_type=F32
        ) + lax.dot_general(keys, rows_low, NT, preferred_element_type=F32)
        return carry

    one_level(0, 0)
    for side in range(2):
        rim(LATENT, side).start()
    lax.fori_loop(1, LEVELS, one_level, 0)

    top = logits[0]
    for l in range(1, LEVELS):
        top = jnp.maximum(top, logits[l])
    norm = jnp.zeros_like(top)
    for l in range(LEVELS):
        power = jnp.exp(logits[l] - top)
        logits[l] = power
        norm = norm + power
    scale = 1.0 / norm

    wide_row = lax.broadcasted_iota(jnp.int32, (4 * HEADS, LATENT * width), 0)
    wide_lane = lax.broadcasted_iota(jnp.int32, (4 * HEADS, LATENT * width), 1) // head
    expand = jnp.where(wide_row == wide_lane, 1.0, 0.0).astype(BF16)
    gath[...] = jnp.zeros_like(gath)

    def weigh(l, carry):
        attn = (logits[l] * scale).astype(BF16)
        value = pair[l].astype(F32)
        wide = jnp.dot(attn, expand, preferred_element_type=F32)
        for j in range(LATENT):
            gath[j] += wide[:, j * width:(j + 1) * width] * value
        return carry

    lax.fori_loop(0, LEVELS, weigh, 0)

    def project_own(j):
        own_triple[j * patches:(j + 1) * patches, :] = jnp.dot(
            normed_ref[j], qkv_ref[...], preferred_element_type=F32
        ).astype(BF16)

    for j in range(LATENT):
        finish_level(j, latents[j:j + 1, :].astype(F32) + jnp.dot(
            gath[j].astype(BF16), perc_out[...], preferred_element_type=F32
        ))
        if j:
            for side in range(2):
                rim(j - 1, side).start()
    project_own(LATENT)
    for side in range(2):
        rim(LATENT - 1, side).start()
    for j in range(LATENT):
        project_own(j)

    first = shift_ref[0]
    column = lax.broadcasted_iota(jnp.int32, (patches, width), 0) % WW
    for j in (LATENT,) + tuple(range(LATENT)):
        for side in range(2):
            rim(j, side).wait_recv()
        near = jnp.where(
            column >= first, left_ref[j].astype(F32), right_ref[j].astype(F32)
        ).astype(BF16)
        near_pair[j * patches:(j + 1) * patches, :] = jnp.dot(
            near, qkv_ref[:, width:], preferred_element_type=F32
        ).astype(BF16)

    levels = LATENT + 1
    members = WL * patches
    q_first = lax.broadcasted_iota(jnp.int32, (members, members), 0) % WW < first
    k_first = lax.broadcasted_iota(jnp.int32, (members, members), 1) % WW < first
    same = q_first == k_first
    half_lane = lax.broadcasted_iota(jnp.int32, (members, 2 * head), 1) // head
    root = 1.0 / math.sqrt(head)
    for g in range(levels // WL):
        r = slice(g * members, (g + 1) * members)
        for h2 in range(HEADS // 2):
            c = slice(h2 * 2 * head, (h2 + 1) * 2 * head)
            ck = slice(width + h2 * 2 * head, width + (h2 + 1) * 2 * head)
            cv = slice(2 * width + h2 * 2 * head, 2 * width + (h2 + 1) * 2 * head)
            q = own_triple[r, c]
            k_own = own_triple[r, ck]
            v_own = own_triple[r, cv]
            k_near = near_pair[r, c]
            v_near = near_pair[r, ck]
            halves = []
            for one in range(2):
                q_one = jnp.where(half_lane == one, q, jnp.zeros_like(q))
                a = lax.dot_general(q_one, k_own, NT, preferred_element_type=F32) * root
                b = lax.dot_general(q_one, k_near, NT, preferred_element_type=F32) * root
                a = jnp.where(same, a, -jnp.inf)
                b = jnp.where(same, -jnp.inf, b)
                peak = jnp.maximum(
                    jnp.max(a, axis=-1, keepdims=True), jnp.max(b, axis=-1, keepdims=True)
                )
                a = jnp.exp(a - peak)
                b = jnp.exp(b - peak)
                unit = 1.0 / (
                    jnp.sum(a, axis=-1, keepdims=True) + jnp.sum(b, axis=-1, keepdims=True)
                )
                halves.append(
                    jnp.dot((a * unit).astype(BF16), v_own, preferred_element_type=F32)
                    + jnp.dot((b * unit).astype(BF16), v_near, preferred_element_type=F32)
                )
            mixed_ref[r, c] = jnp.where(half_lane == 0, halves[0], halves[1]).astype(BF16)
        result = jnp.dot(mixed_ref[r, :], out_w_ref[...], preferred_element_type=F32)
        for level in range(WL):
            j = g * WL + level
            full = state_ref[j] + result[level * patches:(level + 1) * patches, :]
            for i in range(WH):
                out_ref[j, 0, i] = full[i * WW:(i + 1) * WW, :].astype(BF16)

    def drain(k, carry):
        copy(k).wait_send()
        table_copy(k).wait_send()
        return carry

    lax.fori_loop(1, n, drain, 0)
    for j in range(levels):
        for side in range(2):
            rim(j, side).wait_send()


def local(
    pixels, channel_index_table, group_sizes, patch_weight, patch_bias, level_code, latents,
    perc_query, perc_kv, perc_out, norm_gain, window_qkv, window_out, shift,
):
    n = lax.axis_size("tile")
    cap, pix, all_patches = pixels.shape
    patches = all_patches // n
    kind_count, _, width = patch_weight.shape
    levels = LATENT + 1
    vmem = pl.BlockSpec(memory_space=pltpu.VMEM)
    smem = pl.BlockSpec(memory_space=pltpu.SMEM)

    slot = jnp.arange(cap, dtype=jnp.int32)[None, :]
    marked = jnp.where(
        slot < group_sizes[:, None], channel_index_table, channel_index_table + CHANNELS
    )
    marked = jnp.pad(marked, ((0, 0), (0, 128 - cap)), constant_values=-1)
    blocks = pixels.reshape(cap * pix, all_patches).T.reshape(n, patches, cap * pix)
    inverse_shape = (-(-CHANNELS // 8) * 8, 128)
    return pl.pallas_call(
        functools.partial(encode, n, cap),
        out_shape=jax.ShapeDtypeStruct((levels, 1, WH, patches // WH, width), BF16),
        in_specs=[smem] + [vmem] * 12,
        out_specs=vmem,
        scratch_shapes=[
            pltpu.VMEM((n, patches, cap * pix), BF16),
            pltpu.VMEM((n * cap, patches, width), BF16),
            pltpu.VMEM((LEVELS, patches, width), BF16),
            pltpu.VMEM((LEVELS, patches, 4 * HEADS), F32),
            pltpu.VMEM((LATENT, patches, width), F32),
            pltpu.VMEM((n, 1, 128), jnp.int32),
            pltpu.VMEM(inverse_shape, jnp.int32),
            pltpu.SMEM((n, 1, 128), jnp.int32),
            pltpu.SMEM(inverse_shape, jnp.int32),
            pltpu.VMEM((kind_count, 1, width), F32),
            pltpu.VMEM((LEVELS + 1, 1, width), F32),
            pltpu.VMEM((levels, patches, width), F32),
            pltpu.VMEM((levels, patches, width), BF16),
            pltpu.VMEM((levels, patches, width), BF16),
            pltpu.VMEM((levels, patches, width), BF16),
            pltpu.VMEM((levels * patches, 3 * width), BF16),
            pltpu.VMEM((levels * patches, 2 * width), BF16),
            pltpu.VMEM((levels * patches, width), BF16),
            pltpu.SemaphoreType.DMA((n,)),
            pltpu.SemaphoreType.DMA((n,)),
            pltpu.SemaphoreType.DMA((n,)),
            pltpu.SemaphoreType.DMA((n,)),
            pltpu.SemaphoreType.DMA((2,)),
            pltpu.SemaphoreType.DMA((levels, 2)),
            pltpu.SemaphoreType.DMA((levels, 2)),
        ],
        compiler_params=pltpu.CompilerParams(
            collective_id=0, has_side_effects=True, vmem_limit_bytes=60 * 1024 * 1024
        ),
    )(
        shift, marked, blocks, patch_weight, patch_bias, level_code, latents, perc_query,
        perc_kv, perc_out, norm_gain.reshape(1, width), window_qkv, window_out,
    )


def solution(mesh):
    in_specs = (P("tile", "member", None), P("tile", None), P("tile")) + (P(),) * 11
    out_specs = P(None, "tile", "member", None, None)
    return jax.shard_map(local, mesh=mesh, in_specs=in_specs, out_specs=out_specs, check_vma=False)
```

time: 153 us -> 116 us (0.76)
  the two profiles are of different devices: /device:TPU:16 before, /device:TPU:12 now
where the time goes in v2:
time: 116 us
  Pallas kernels  105 us (91%)
  local copies, waits for them, and re-layouts  9.2 us (8%)
  between operations  1.31 us (1%)
    pallas_call x1, Pallas kernels, local(): pl.pallas_call(functools.partial(encode, n, cap), out_shape=jax.ShapeDtyp...  105 us
    reshape x1, local copies, waits for them, and re-layouts, local(): pixels.reshape(cap * pix, all_patches).T.reshape(n, patches, cap * pix)  5.41 us

profile of v2, /device:TPU:12, one launch (start us, length us, event | category | flops | bytes accessed | tf_op | source)
XLA Modules:
  0.0 115.9 jit_solution(12327564951233713388)
XLA Ops:
  1.3 0.7 compare_select_fusion
  2.0 0.6 pad.4.marked_ref
  2.5 1.3 %reshape.22.gain = bf16[1,512]{1,0:T(2,128)(2,1)} reshape(bf16[512]{0:T(512)(128)(2,1)} %param.24) | data formatting | bytes 2048 | tf_op jit(solution)/shard_map/reshape | solution.py:359
  3.8 5.4 %copy.15 = bf16[1200,1152]{0,1:T(8,128)(2,1)} copy(bf16[1200,1152]{1,0:T(8,128)(2,1)} %bitcast.7) | data formatting | bytes 5529600 | tf_op jit(solution)/shard_map/reshape | solution.py:320
  9.2 104.7 %shard_map.136 = bf16[4,1,6,12,512]{4,3,2,1,0:T(8,128)(2,1)} custom-call(s32[1]{0:T(128)S(6)} %copy.18.shift_ref, s32[1,128]{1,0:T(1,128)} %pad.4.marked_ref, bf16[16,72,1200]{2,1,0:T(8,128)(2,1)} %bitcast.6, bf16[9,200,512]{2,1,0:T(8,128)(2,1)} %weight.1, bf16[9,512]{1,0:T(8,128)(2,1)} %bias.1, bf16[14,512]{1,0:T(8,128)(2,1)} %code.1, ...), custom_call_target="tpu_custom_call" | custom-call | tf_op jit(solution)/shard_map/pallas_call | solution.py:322
  114.0 1.9 %copy.16 = bf16[4,1,6,12,512]{4,0,3,2,1:T(4,128)(2,1)} copy(bf16[4,1,6,12,512]{4,3,2,1,0:T(8,128)(2,1)} %shard_map.136) | data formatting | bytes 589824 | tf_op jit(solution)/shard_map/pallas_call | solution.py:322

commit v3 on v2

--- a/solution.py
+++ b/solution.py
@@ -24,12 +24,17 @@
 
 
 def encode(
-    n, cap, shift_ref, marked_ref, x_ref, weight, bias, code, latents, perc_query, perc_kv,
-    perc_out, gain, qkv_ref, out_w_ref, out_ref, recv, emb, pair, logits, gath, recv_ids,
+    n, cap, shift_ref, sizes_ref, table_ref, bias, code, latents, gain, x_ref, *refs
+):
+    hbm_weights, (out_ref, marked_ref), refs = refs[:6], refs[6:8], refs[8:]
+    vmem_weights, refs = refs[:6], refs[6:]
+    weight, perc_query, perc_kv, perc_out, qkv_ref, out_w_ref = vmem_weights
+    (
+    recv, emb, pair, logits, recv_ids,
     inverse, ids, slot_of, bias_rows, code_rows, state_ref, normed_ref, left_ref, right_ref,
     own_triple, near_pair, mixed_ref, send_sem, recv_sem, table_send, table_recv, local_sem,
-    rim_send, rim_recv,
-):
+    rim_send, rim_recv, weight_sem,
+    ) = refs
     me = lax.axis_index("tile")
     bands = n // LT
     patches, packed = x_ref.shape[1:]
@@ -44,6 +49,18 @@
         return carry
 
     lax.fori_loop(1, n, greet, 0)
+    fetches = [
+        pltpu.make_async_copy(source, target, weight_sem.at[i])
+        for i, (source, target) in enumerate(zip(hbm_weights, vmem_weights))
+    ]
+    for fetch in fetches[:2]:
+        fetch.start()
+    own_block = pltpu.make_async_copy(x_ref.at[me], recv.at[me], local_sem.at[2])
+    own_block.start()
+    lane = lax.broadcasted_iota(jnp.int32, (1, cap), 1)
+    table = table_ref[...]
+    marked_ref[...] = jnp.full(marked_ref.shape, -1, jnp.int32)
+    marked_ref[:, :cap] = jnp.where(lane < sizes_ref[0], table, table + CHANNELS)
     pl.semaphore_wait(barrier, n - 1)
 
     def offset(i):
@@ -82,12 +99,15 @@
 
     lax.fori_loop(0, n - 1, launch_block, 0)
 
+    for fetch in fetches[2:]:
+        fetch.start()
     recv_ids[me] = marked_ref[...]
     for i in range(bias.shape[0]):
         bias_rows[i] = bias[i:i + 1, :].astype(F32)
     for i in range(code.shape[0]):
         code_rows[i] = code[i:i + 1, :].astype(F32)
 
+    fetches[1].wait()
     query = jnp.dot(latents[...], perc_query[...], preferred_element_type=F32) / math.sqrt(head)
     lane_head = lax.broadcasted_iota(jnp.int32, (HEADS, width), 1) // head
     row_head = lax.broadcasted_iota(jnp.int32, (HEADS, width), 0)
@@ -131,7 +151,9 @@
             )
             emb[source * cap + s] = (value + bias_rows[kind]).astype(BF16)
 
-    embed(x_ref[me], me)
+    fetches[0].wait()
+    own_block.wait()
+    embed(recv[me], me)
     to_slots = pltpu.make_async_copy(inverse, slot_of, local_sem.at[1])
     to_slots.start()
     to_slots.wait()
@@ -143,6 +165,8 @@
         embed(recv[source], source)
         return carry
 
+    for fetch in fetches[2:]:
+        fetch.wait()
     lax.fori_loop(0, n - 1, land, 0)
 
     def channel_value(c):
@@ -158,12 +182,14 @@
             device_id={"tile": to},
         )
 
+    gain_row = gain[...].astype(F32).reshape(1, width)
+
     def finish_level(j, state):
         center = state - jnp.mean(state, axis=-1, keepdims=True)
         spread_of = jnp.mean(center * center, axis=-1, keepdims=True)
         state_ref[j] = state
         normed_ref[j] = (
-            center * lax.rsqrt(spread_of + 1e-05) * gain[...].astype(F32)
+            center * lax.rsqrt(spread_of + 1e-05) * gain_row
         ).astype(BF16)
 
     surface = channel_value(V_ATM * LEVELS)
@@ -199,42 +225,18 @@
         norm = norm + power
     scale = 1.0 / norm
 
-    wide_row = lax.broadcasted_iota(jnp.int32, (4 * HEADS, LATENT * width), 0)
-    wide_lane = lax.broadcasted_iota(jnp.int32, (4 * HEADS, LATENT * width), 1) // head
-    expand = jnp.where(wide_row == wide_lane, 1.0, 0.0).astype(BF16)
-    gath[...] = jnp.zeros_like(gath)
-
-    def weigh(l, carry):
-        attn = (logits[l] * scale).astype(BF16)
-        value = pair[l].astype(F32)
-        wide = jnp.dot(attn, expand, preferred_element_type=F32)
-        for j in range(LATENT):
-            gath[j] += wide[:, j * width:(j + 1) * width] * value
-        return carry
-
-    lax.fori_loop(0, LEVELS, weigh, 0)
+    wide_row = lax.broadcasted_iota(jnp.int32, (4 * HEADS, width), 0)
+    wide_lane = lax.broadcasted_iota(jnp.int32, (4 * HEADS, width), 1) // head
 
     def project_own(j):
         own_triple[j * patches:(j + 1) * patches, :] = jnp.dot(
             normed_ref[j], qkv_ref[...], preferred_element_type=F32
         ).astype(BF16)
 
-    for j in range(LATENT):
-        finish_level(j, latents[j:j + 1, :].astype(F32) + jnp.dot(
-            gath[j].astype(BF16), perc_out[...], preferred_element_type=F32
-        ))
-        if j:
-            for side in range(2):
-                rim(j - 1, side).start()
-    project_own(LATENT)
-    for side in range(2):
-        rim(LATENT - 1, side).start()
-    for j in range(LATENT):
-        project_own(j)
-
     first = shift_ref[0]
     column = lax.broadcasted_iota(jnp.int32, (patches, width), 0) % WW
-    for j in (LATENT,) + tuple(range(LATENT)):
+
+    def project_near(j):
         for side in range(2):
             rim(j, side).wait_recv()
         near = jnp.where(
@@ -244,6 +246,22 @@
             near, qkv_ref[:, width:], preferred_element_type=F32
         ).astype(BF16)
 
+    for l in range(LEVELS):
+        logits[l] = (logits[l] * scale).astype(BF16).astype(F32)
+    for j in range(LATENT):
+        expand = jnp.where(wide_row == wide_lane + j * HEADS, 1.0, 0.0).astype(BF16)
+        gathered = jnp.zeros((patches, width), F32)
+        for l in range(LEVELS):
+            wide = jnp.dot(logits[l].astype(BF16), expand, preferred_element_type=F32)
+            gathered = gathered + wide * pair[l].astype(F32)
+        finish_level(j, latents[j:j + 1, :].astype(F32) + jnp.dot(
+            gathered.astype(BF16), perc_out[...], preferred_element_type=F32
+        ))
+        project_own(j)
+        for side in range(2):
+            rim(j, side).start()
+    project_own(LATENT)
+
     levels = LATENT + 1
     members = WL * patches
     q_first = lax.broadcasted_iota(jnp.int32, (members, members), 0) % WW < first
@@ -252,6 +270,8 @@
     half_lane = lax.broadcasted_iota(jnp.int32, (members, 2 * head), 1) // head
     root = 1.0 / math.sqrt(head)
     for g in range(levels // WL):
+        for level in reversed(range(WL)):
+            project_near(g * WL + level)
         r = slice(g * members, (g + 1) * members)
         for h2 in range(HEADS // 2):
             c = slice(h2 * 2 * head, (h2 + 1) * 2 * head)
@@ -267,19 +287,18 @@
                 q_one = jnp.where(half_lane == one, q, jnp.zeros_like(q))
                 a = lax.dot_general(q_one, k_own, NT, preferred_element_type=F32) * root
                 b = lax.dot_general(q_one, k_near, NT, preferred_element_type=F32) * root
-                a = jnp.where(same, a, -jnp.inf)
-                b = jnp.where(same, -jnp.inf, b)
-                peak = jnp.maximum(
-                    jnp.max(a, axis=-1, keepdims=True), jnp.max(b, axis=-1, keepdims=True)
-                )
-                a = jnp.exp(a - peak)
-                b = jnp.exp(b - peak)
-                unit = 1.0 / (
-                    jnp.sum(a, axis=-1, keepdims=True) + jnp.sum(b, axis=-1, keepdims=True)
-                )
+                both = jnp.where(same, a, b)
+                both = jnp.exp(both - jnp.max(both, axis=-1, keepdims=True))
+                both = both * (1.0 / jnp.sum(both, axis=-1, keepdims=True))
                 halves.append(
-                    jnp.dot((a * unit).astype(BF16), v_own, preferred_element_type=F32)
-                    + jnp.dot((b * unit).astype(BF16), v_near, preferred_element_type=F32)
+                    jnp.dot(
+                        jnp.where(same, both, 0.0).astype(BF16), v_own,
+                        preferred_element_type=F32,
+                    )
+                    + jnp.dot(
+                        jnp.where(same, 0.0, both).astype(BF16), v_near,
+                        preferred_element_type=F32,
+                    )
                 )
             mixed_ref[r, c] = jnp.where(half_lane == 0, halves[0], halves[1]).astype(BF16)
         result = jnp.dot(mixed_ref[r, :], out_w_ref[...], preferred_element_type=F32)
@@ -311,25 +330,23 @@
     levels = LATENT + 1
     vmem = pl.BlockSpec(memory_space=pltpu.VMEM)
     smem = pl.BlockSpec(memory_space=pltpu.SMEM)
-
-    slot = jnp.arange(cap, dtype=jnp.int32)[None, :]
-    marked = jnp.where(
-        slot < group_sizes[:, None], channel_index_table, channel_index_table + CHANNELS
-    )
-    marked = jnp.pad(marked, ((0, 0), (0, 128 - cap)), constant_values=-1)
+    stays = pl.BlockSpec(memory_space=pl.ANY)
+    weights = (patch_weight, perc_query, perc_kv, perc_out, window_qkv, window_out)
+
     blocks = pixels.reshape(cap * pix, all_patches).T.reshape(n, patches, cap * pix)
     inverse_shape = (-(-CHANNELS // 8) * 8, 128)
     return pl.pallas_call(
         functools.partial(encode, n, cap),
         out_shape=jax.ShapeDtypeStruct((levels, 1, WH, patches // WH, width), BF16),
-        in_specs=[smem] + [vmem] * 12,
+        in_specs=[smem] * 2 + [vmem] * 5 + [stays] * 7,
         out_specs=vmem,
         scratch_shapes=[
+            pltpu.VMEM((1, 128), jnp.int32),
+            *[pltpu.VMEM(w.shape, BF16) for w in weights],
             pltpu.VMEM((n, patches, cap * pix), BF16),
             pltpu.VMEM((n * cap, patches, width), BF16),
             pltpu.VMEM((LEVELS, patches, width), BF16),
             pltpu.VMEM((LEVELS, patches, 4 * HEADS), F32),
-            pltpu.VMEM((LATENT, patches, width), F32),
             pltpu.VMEM((n, 1, 128), jnp.int32),
             pltpu.VMEM(inverse_shape, jnp.int32),
             pltpu.SMEM((n, 1, 128), jnp.int32),
@@ -347,16 +364,17 @@
             pltpu.SemaphoreType.DMA((n,)),
             pltpu.SemaphoreType.DMA((n,)),
             pltpu.SemaphoreType.DMA((n,)),
-            pltpu.SemaphoreType.DMA((2,)),
+            pltpu.SemaphoreType.DMA((3,)),
             pltpu.SemaphoreType.DMA((levels, 2)),
             pltpu.SemaphoreType.DMA((levels, 2)),
+            pltpu.SemaphoreType.DMA((len(weights),)),
         ],
         compiler_params=pltpu.CompilerParams(
             collective_id=0, has_side_effects=True, vmem_limit_bytes=60 * 1024 * 1024
         ),
     )(
-        shift, marked, blocks, patch_weight, patch_bias, level_code, latents, perc_query,
-        perc_kv, perc_out, norm_gain.reshape(1, width), window_qkv, window_out,
+        shift, group_sizes, channel_index_table, patch_bias, level_code, latents, norm_gain,
+        blocks, *weights,
     )
 
 

time: 116 us -> 111 us (0.957)
  Pallas kernels: 105 us -> 102 us
  local copies, waits for them, and re-layouts: 9.2 us -> 7.37 us
    pallas_call x1, Pallas kernels: 105 us -> 102 us  [local(): pl.pallas_call(functools.partial(encode, n, cap), out_shape=jax.ShapeDtyp...]
    reshape x1 -> x0, local copies, waits for them, and re-layouts: 1.26 us -> none  [local(): norm_gain.reshape(1, width)]
where the time goes in v3:
time: 111 us
  Pallas kernels  102 us (92%)
  local copies, waits for them, and re-layouts  7.37 us (7%)
  between operations  1.31 us (1%)
    pallas_call x1, Pallas kernels, local(): pl.pallas_call(functools.partial(encode, n, cap), out_shape=jax.ShapeDtyp...  102 us
    reshape x1, local copies, waits for them, and re-layouts, local(): pixels.reshape(cap * pix, all_patches).T.reshape(n, patches, cap * pix)  5.42 us

profile of v3, /device:TPU:12, one launch (start us, length us, event | category | flops | bytes accessed | tf_op | source)
XLA Modules:
  0.0 110.8 jit_solution(2798131169533853088)
XLA Ops:
  1.3 5.4 %copy.15 = bf16[1200,1152]{0,1:T(8,128)(2,1)} copy(bf16[1200,1152]{1,0:T(8,128)(2,1)} %bitcast.5) | data formatting | bytes 5529600 | tf_op jit(solution)/shard_map/reshape | solution.py:336
  6.7 102.2 %shard_map.136 = bf16[4,1,6,12,512]{4,3,2,1,0:T(8,128)(2,1)} custom-call(s32[1]{0:T(128)S(6)} %copy.18.shift_ref, s32[1]{0:T(128)S(6)} %copy.17.sizes_ref, s32[1,6]{1,0:T(1,128)} %table_ref.1, bf16[9,512]{1,0:T(8,128)(2,1)} %bias.1, bf16[14,512]{1,0:T(8,128)(2,1)} %code.1, bf16[3,512]{1,0:T(4,128)(2,1)} %latents.1, bf16[512]{0:T(512)(128)(2,1)} %gain.1, ...), custom_call_target="tpu_custom_call" | custom-call | tf_op jit(solution)/shard_map/pallas_call | solution.py:338
  108.9 1.9 %copy.16 = bf16[4,1,6,12,512]{4,0,3,2,1:T(4,128)(2,1)} copy(bf16[4,1,6,12,512]{4,3,2,1,0:T(8,128)(2,1)} %shard_map.136) | data formatting | bytes 589824 | tf_op jit(solution)/shard_map/pallas_call | solution.py:338

commit v4 on v3

--- a/solution.py
+++ b/solution.py
@@ -33,7 +33,7 @@
     recv, emb, pair, logits, recv_ids,
     inverse, ids, slot_of, bias_rows, code_rows, state_ref, normed_ref, left_ref, right_ref,
     own_triple, near_pair, mixed_ref, send_sem, recv_sem, table_send, table_recv, local_sem,
-    rim_send, rim_recv, weight_sem,
+    rim_send, rim_recv, weight_sem, tokens,
     ) = refs
     me = lax.axis_index("tile")
     bands = n // LT
@@ -197,23 +197,21 @@
         surface = surface + channel_value(c)
     finish_level(LATENT, surface + code_rows[LEVELS])
 
-    def one_level(l, carry):
+    for l in range(LEVELS):
         total = channel_value(l)
         for v in range(1, V_ATM):
             total = total + channel_value(v * LEVELS + l)
-        token = (total + code_rows[l]).astype(BF16)
-        both = jnp.dot(token, perc_kv[...], preferred_element_type=F32).astype(BF16)
-        pair[l] = both[:, width:]
-        keys = both[:, :width]
-        logits[l] = lax.dot_general(
-            keys, rows_high, NT, preferred_element_type=F32
-        ) + lax.dot_general(keys, rows_low, NT, preferred_element_type=F32)
-        return carry
-
-    one_level(0, 0)
+        tokens[l * patches:(l + 1) * patches, :] = (total + code_rows[l]).astype(BF16)
     for side in range(2):
         rim(LATENT, side).start()
-    lax.fori_loop(1, LEVELS, one_level, 0)
+    keys = jnp.dot(tokens[...], perc_kv[:, :width], preferred_element_type=F32).astype(BF16)
+    scores = lax.dot_general(
+        keys, rows_high, NT, preferred_element_type=F32
+    ) + lax.dot_general(keys, rows_low, NT, preferred_element_type=F32)
+    values = jnp.dot(tokens[...], perc_kv[:, width:], preferred_element_type=F32).astype(BF16)
+    for l in range(LEVELS):
+        logits[l] = scores[l * patches:(l + 1) * patches, :]
+        pair[l] = values[l * patches:(l + 1) * patches, :]
 
     top = logits[0]
     for l in range(1, LEVELS):
@@ -368,6 +366,7 @@
             pltpu.SemaphoreType.DMA((levels, 2)),
             pltpu.SemaphoreType.DMA((levels, 2)),
             pltpu.SemaphoreType.DMA((len(weights),)),
+            pltpu.VMEM((LEVELS * patches, width), BF16),
         ],
         compiler_params=pltpu.CompilerParams(
             collective_id=0, has_side_effects=True, vmem_limit_bytes=60 * 1024 * 1024

time: 111 us -> 107 us (0.964)
  Pallas kernels: 102 us -> 98.3 us
    pallas_call x1, Pallas kernels: 102 us -> 98.3 us  [local(): pl.pallas_call(functools.partial(encode, n, cap), out_shape=jax.ShapeDtyp...]
where the time goes in v4:
time: 107 us
  Pallas kernels  98.3 us (92%)
  local copies, waits for them, and re-layouts  7.37 us (7%)
  between operations  1.31 us (1%)
    pallas_call x1, Pallas kernels, local(): pl.pallas_call(functools.partial(encode, n, cap), out_shape=jax.ShapeDtyp...  98.3 us
    reshape x1, local copies, waits for them, and re-layouts, local(): pixels.reshape(cap * pix, all_patches).T.reshape(n, patches, cap * pix)  5.42 us

profile of v4, /device:TPU:12, one launch (start us, length us, event | category | flops | bytes accessed | tf_op | source)
XLA Modules:
  0.0 107.0 jit_solution(11210351301679466240)
XLA Ops:
  1.3 5.4 %copy.15 = bf16[1200,1152]{0,1:T(8,128)(2,1)} copy(bf16[1200,1152]{1,0:T(8,128)(2,1)} %bitcast.5) | data formatting | bytes 5529600 | tf_op jit(solution)/shard_map/reshape | solution.py:334
  6.7 98.3 %shard_map.136 = bf16[4,1,6,12,512]{4,3,2,1,0:T(8,128)(2,1)} custom-call(s32[1]{0:T(128)S(6)} %copy.18.shift_ref, s32[1]{0:T(128)S(6)} %copy.17.sizes_ref, s32[1,6]{1,0:T(1,128)} %table_ref.1, bf16[9,512]{1,0:T(8,128)(2,1)} %bias.1, bf16[14,512]{1,0:T(8,128)(2,1)} %code.1, bf16[3,512]{1,0:T(4,128)(2,1)} %latents.1, bf16[512]{0:T(512)(128)(2,1)} %gain.1, ...), custom_call_target="tpu_custom_call" | custom-call | tf_op jit(solution)/shard_map/pallas_call | solution.py:336
  105.1 1.9 %copy.16 = bf16[4,1,6,12,512]{4,0,3,2,1:T(4,128)(2,1)} copy(bf16[4,1,6,12,512]{4,3,2,1,0:T(8,128)(2,1)} %shard_map.136) | data formatting | bytes 589824 | tf_op jit(solution)/shard_map/pallas_call | solution.py:336
